TPU v7x, 32 devices: a whole 2x2x4 slice. The times are simulated.
32 devices in a mesh: fsdp: 4 (over y, x), rep: 8 (over z, core).
Axes of the slice: x: 2, y: 2, z: 4, core: 2. Of those that a mesh axis runs over, the one named last changes fastest.
Arguments:
- hidden_in: bfloat16 [8192, 2048], P(('fsdp', 'rep'))
- out_grad: bfloat16 [8192, 2048], P(('fsdp', 'rep')), may hold values from -6 to 6
- attn_saved: bfloat16 [8192, 256], P(('fsdp', 'rep')), may hold values from -6 to 6
- row_lse: float32 [8192, 2], P(('fsdp', 'rep')), may hold values from 2.5 to 6
- w_qkv: bfloat16 [2048, 512], P('fsdp'), may hold values from -0.125 to 0.125
- w_out_t: bfloat16 [2048, 256], P('fsdp'), may hold values from -0.125 to 0.125
- doc_lengths: int32 [32, 4], P(('fsdp', 'rep')), may hold values from 1 to 128, 256 in all within a row
- seq_start: int32 [32], P(('fsdp', 'rep')), may hold values from 0 to 2047
Outputs:
- input_grad: bfloat16 [8192, 2048], P(('fsdp', 'rep'))
- grad_update: float32 [2048, 768], P('fsdp')
- grad_norm: float32 [], replicated
Inputs may be any that keep to these rules, and one draw needn't show every extreme that they name: `doc_lengths`: each row sums to 256; the longest document of each device has exactly 128 tokens.
All inputs are finite; a program needn't handle non-finite values.
Results may differ from a plain program's by a relative error of at most 0.014.
Values may be sent and summed in bfloat16 or wider, within the bound.
A program may use at most 64 MiB of HBM per device.

v0:
```python
import jax
import jax.numpy as jnp
from jax import lax
from jax.sharding import PartitionSpec as P

D = 2048
HEAD = 128


def rotary(values_in, positions, turn, head_size):
    rows = values_in.shape[0]
    heads_count = values_in.shape[1] // head_size
    half_size = head_size // 2
    inverse = 1000000.0 ** (-(jnp.arange(half_size, dtype=jnp.float32) * 2.0) / head_size)
    angles = positions.astype(jnp.float32)[:, None] * inverse[None, :]
    cosine = jnp.cos(angles)[:, None, :]
    sines = jnp.sin(angles)[:, None, :]
    shaped = values_in.reshape(rows, heads_count, head_size)
    first_half = shaped[:, :, :half_size]
    second_half = shaped[:, :, half_size:]
    result = jnp.concatenate(
        [
            first_half * cosine - turn * second_half * sines,
            second_half * cosine + turn * first_half * sines,
        ],
        axis=2,
    )
    return result.reshape(rows, heads_count * head_size)


def contract_rows(left, right):
    return lax.dot_general(
        left, right, (((0,), (0,)), ((), ())), preferred_element_type=jnp.float32
    )


def contract_cols(left, right):
    return lax.dot_general(
        left, right, (((1,), (1,)), ((), ())), preferred_element_type=jnp.float32
    )


def body(hidden_in, out_grad, attn_saved, row_lse, w_qkv, w_out_t, doc_lengths, seq_start):
    seq_rows = hidden_in.shape[0]
    head_size = HEAD
    query_width = attn_saved.shape[1]
    heads_count = row_lse.shape[1]
    scale = 1.0 / head_size**0.5
    tokens_part = hidden_in
    grads_part = out_grad
    proj = jnp.dot(
        tokens_part,
        lax.all_gather(w_qkv, "fsdp", axis=0, tiled=True),
        preferred_element_type=jnp.float32,
    )
    attn_full = jnp.dot(
        grads_part,
        lax.all_gather(w_out_t, "fsdp", axis=0, tiled=True),
        preferred_element_type=jnp.float32,
    )
    attn_grad = attn_full.astype(jnp.bfloat16)
    positions = seq_start[0] + jnp.arange(seq_rows, dtype=jnp.int32)
    queries = rotary(proj[:, :query_width], positions, 1.0, head_size).astype(jnp.bfloat16)
    keys = rotary(proj[:, query_width : query_width + head_size], positions, 1.0, head_size).astype(
        jnp.bfloat16
    )
    values_all = proj[:, query_width + head_size :].astype(jnp.bfloat16)
    ends = jnp.cumsum(doc_lengths[0])
    local_rows = jnp.arange(seq_rows, dtype=jnp.int32)
    documents = jnp.sum((local_rows[:, None] >= ends[None, :]).astype(jnp.int32), axis=1)
    block_rows = min(seq_rows, 512)
    block_count = seq_rows // block_rows

    def attend_block(carry, inputs):
        key_grad, value_grad = carry
        query_rows, grad_rows, saved_rows, lse_rows, index_rows, doc_rows = inputs
        allowed = (doc_rows[:, None] == documents[None, :]) & (
            local_rows[None, :] <= index_rows[:, None]
        )
        query_parts = []
        for head_index in range(heads_count):
            lower = head_index * head_size
            query_head = query_rows[:, lower : lower + head_size]
            scores = contract_cols(query_head, keys) * scale
            probs = jnp.where(
                allowed, jnp.exp(scores - lse_rows[:, head_index : head_index + 1]), 0.0
            )
            grad_head = grad_rows[:, lower : lower + head_size]
            dprobs = contract_cols(grad_head, values_all)
            delta = jnp.sum(
                grad_head.astype(jnp.float32)
                * saved_rows[:, lower : lower + head_size].astype(jnp.float32),
                axis=1,
                keepdims=True,
            )
            dscores = (probs * (dprobs - delta) * scale).astype(jnp.bfloat16)
            probs_low = probs.astype(jnp.bfloat16)
            value_grad = value_grad + contract_rows(probs_low, grad_head)
            query_parts.append(jnp.dot(dscores, keys, preferred_element_type=jnp.float32))
            key_grad = key_grad + contract_rows(dscores, query_head)
        return ((key_grad, value_grad), jnp.concatenate(query_parts, axis=1))

    block_inputs = (
        queries.reshape(block_count, block_rows, query_width),
        attn_grad.reshape(block_count, block_rows, query_width),
        attn_saved.reshape(block_count, block_rows, query_width),
        row_lse.reshape(block_count, block_rows, heads_count),
        local_rows.reshape(block_count, block_rows),
        documents.reshape(block_count, block_rows),
    )
    zero_grad = jnp.zeros((seq_rows, head_size), jnp.float32)
    (key_grad, value_grad), query_blocks = lax.scan(
        attend_block, (zero_grad, zero_grad), block_inputs
    )
    query_grad = rotary(
        query_blocks.reshape(seq_rows, query_width), positions, -1.0, head_size
    ).astype(jnp.bfloat16)
    key_grad = rotary(key_grad, positions, -1.0, head_size).astype(jnp.bfloat16)
    d_qkv = jnp.concatenate([query_grad, key_grad, value_grad.astype(jnp.bfloat16)], axis=1)
    input_full = contract_cols(d_qkv, lax.all_gather(w_qkv, "fsdp", axis=0, tiled=True))
    input_grad = input_full.astype(jnp.bfloat16)
    tokens_part = hidden_in
    grads_part = out_grad
    shard_sum = lax.psum_scatter(
        jnp.concatenate(
            [contract_rows(tokens_part, d_qkv), contract_rows(grads_part, attn_saved)], axis=1
        ).astype(jnp.bfloat16),
        "fsdp",
        scatter_dimension=0,
        tiled=True,
    ).astype(jnp.float32)
    grads = lax.psum(shard_sum, "rep")
    norm_sq = lax.psum(jnp.sum(grads * grads), "fsdp")
    grad_update = grads * lax.rsqrt(norm_sq / (D * grads.shape[1]) + 1e-06)
    return (input_grad, grad_update, jnp.sqrt(norm_sq))


def solution(mesh):
    in_specs = (
        P(("fsdp", "rep"), None),
        P(("fsdp", "rep"), None),
        P(("fsdp", "rep"), None),
        P(("fsdp", "rep"), None),
        P("fsdp", None),
        P("fsdp", None),
        P(("fsdp", "rep"), None),
        P(("fsdp", "rep")),
    )
    out_specs = (P(("fsdp", "rep"), None), P("fsdp", None), P())
    return jax.shard_map(body, mesh=mesh, in_specs=in_specs, out_specs=out_specs, check_vma=False)
```

profile of v0, /device:TPU:0, one launch (start us, length us, event | category | flops | bytes accessed | tf_op | source)
XLA Modules:
  0.0 219.8 jit_solution(17886597577698370556)
XLA Ops:
  7.2 0.7 all-gather.5.cloned.1.call-update
  7.9 0.0 all-gather.3.cloned.1.call-start
  8.0 0.7 all-gather.3.cloned.1.call-update
  8.7 0.0 reduce-scatter.2.cloned.1.call-start
  9.4 0.9 fusion.49
  10.3 0.7 copy.36
  11.0 0.7 copy.37
  11.7 0.8 reduce-window.8
  12.6 0.7 convert_reduce_fusion
  13.2 1.3 fusion.50
  14.6 1.2 broadcast_multiply_fusion.1
  15.8 1.4 convolution_convert_fusion.2
  17.2 21.9 %all-gather.5.cloned.1.call-done = bf16[2048,256]{1,0:T(8,128)(2,1)} async-done(((bf16[512,256]{1,0:T(8,128)(2,1)}), bf16[2048,256]{1,0:T(8,128)(2,1)}) %all-gather.5.cloned.1.call-update) | async-done | bytes 1048592 | tf_op jit(solution)/shard_map/all_gather | solution.py:58
  39.1 1.7 convolution_convert_fusion.3
  40.8 0.9 multiply_reduce_fusion.1
  41.8 34.4 %all-gather.3.cloned.1.call-done = bf16[2048,512]{1,0:T(8,128)(2,1)} async-done(((bf16[512,512]{1,0:T(8,128)(2,1)}), bf16[2048,512]{1,0:T(8,128)(2,1)}) %all-gather.3.cloned.1.call-update) | async-done | bytes 2097168 | tf_op jit(solution)/shard_map/all_gather | solution.py:53
  76.1 2.3 %fusion.51 = f32[256,512]{1,0:T(8,128)S(1)} fusion(bf16[256,2048]{1,0:T(8,128)(2,1)S(1)} %copy-done, bf16[2048,512]{1,0:T(8,128)(2,1)} %all-gather.3.cloned.1.call-done), kind=kOutput, calls=%fused_computation.89 | convolution fusion | flops 536870912 | bytes 3670016 | tf_op jit(solution)/shard_map/dot_general | solution.py:51
  78.5 0.1 copy.35
  78.6 1.0 fusion.28
  79.6 0.1 reshape.176
  79.7 0.5 subtract_convert_fusion.1
  80.2 0.4 pad_maximum_fusion.3
  80.6 1.0 fusion.10
  81.6 0.2 fusion.17
  81.8 0.2 fusion.11
  82.0 0.2 fusion.47
  82.2 0.2 fusion.37
  82.5 0.2 fusion.5
  82.7 0.2 fusion.12
  82.9 0.2 fusion.46
  83.1 0.2 fusion.14
  83.2 0.1 copy.33
  83.4 0.2 fusion.13
  83.6 0.3 fusion.32
  83.9 0.1 copy.32
  84.1 0.1 copy.39
  84.3 0.1 copy.38
  84.4 1.2 subtract_convert_fusion
  85.6 0.4 pad_maximum_fusion.4
  86.0 0.7 fusion
  86.7 1.9 pad_maximum_fusion
  88.7 44.1 %reduce-scatter.2.cloned.1.call-done = bf16[512,768]{0,1:T(8,128)(2,1)} async-done(((bf16[2048,768]{0,1:T(8,128)(2,1)}), bf16[512,768]{0,1:T(8,128)(2,1)}) %reduce-scatter.2.cloned.1.call-update) | async-done | bytes 786448 | tf_op jit(solution)/shard_map/reduce_scatter | solution.py:124
  132.7 59.9 %all-reduce.1 = f32[512,768]{0,1:T(8,128)S(1)} all-reduce(bf16[512,768]{0,1:T(8,128)(2,1)} %reduce-scatter.2.cloned.1.call-done), channel_id=1, replica_groups=mesh['fsdp'=4,'rep'=8] {'rep'}, use_global_device_ids=true, to_apply=%region_5.6 | all-reduce | flops 393216 | bytes 2359296 | tf_op jit(solution)/shard_map/psum | solution.py:132
  192.6 1.0 multiply_reduce_fusion
  193.6 3.3 %convolution_convert_fusion.1 = bf16[256,2048]{1,0:T(8,128)(2,1)} fusion(bf16[2048,512]{1,0:T(8,128)(2,1)} %all-gather.3.cloned.1.call-done, bf16[256,128]{1,0:T(8,128)(2,1)S(1)} %copy.33, bf16[256,128]{1,0:T(8,128)(2,1)S(1)} %copy.32, bf16[256,256]{1,0:T(8,128)(2,1)S(1)} %bitcast.49), kind=kOutput, calls=%fused_computation.3 | convolution fusion | flops 538181632 | bytes 3407872 | tf_op jit(solution)/shard_map/dot_general | solution.py:38
  196.9 9.5 %psum.15 = f32[]{:T(128)} all-reduce(f32[]{:T(128)} %multiply_reduce_fusion), channel_id=1, replica_groups=mesh['fsdp'=4,'rep'=8] {'fsdp'}, use_global_device_ids=true, to_apply=%region_7.8 | all-reduce | flops 1 | bytes 8 | tf_op jit(solution)/shard_map/psum | solution.py:133
  207.8 1.3 broadcast_multiply_fusion
  209.1 3.0 %copy.34 = f32[512,768]{1,0:T(8,128)} copy(f32[512,768]{0,1:T(8,128)} %broadcast_multiply_fusion) | data formatting | bytes 3145728
  (23 shorter events, 0.2 us)
Async XLA Ops:
  7.2 69.0 %copy-start = (bf16[256,2048]{1,0:T(8,128)(2,1)S(1)}, bf16[256,2048]{1,0:T(8,128)(2,1)}, u32[]{:S(2)}) copy-start(bf16[256,2048]{1,0:T(8,128)(2,1)} %param.8) | copy-start | bytes 3145732
  7.2 8.6 %copy-start.1 = (bf16[256,2048]{1,0:T(8,128)(2,1)S(1)}, bf16[256,2048]{1,0:T(8,128)(2,1)}, u32[]{:S(2)}) copy-start(bf16[256,2048]{1,0:T(8,128)(2,1)} %param.9) | copy-start | bytes 3145732
  7.2 31.9 %all-gather.5.cloned.1.call-start = ((), (), s32[]{:S(2)}) async-start(), calls=%async_computation.2 | async-start | bytes 1310720 | tf_op jit(solution)/shard_map/all_gather | solution.py:58
  7.9 68.2 %all-gather.3.cloned.1.call-start = ((), (), s32[]{:S(2)}) async-start(), calls=%async_computation.1 | async-start | bytes 2621440 | tf_op jit(solution)/shard_map/all_gather | solution.py:53
  8.7 124.0 %reduce-scatter.2.cloned.1.call-start = ((), (), s32[]{:S(2)}) async-start(), calls=%async_computation.3 | async-start | bytes 3932160 | tf_op jit(solution)/shard_map/reduce_scatter | solution.py:124
  79.7 2.3 %copy-start.2 = (bf16[256,1,64]{0,2,1:T(8,128)(2,1)S(1)}, bf16[256,1,64]{0,2,1:T(8,128)(2,1)}, u32[]{:S(2)}) copy-start(bf16[256,1,64]{0,2,1:T(8,128)(2,1)} %get-tuple-element.64) | copy-start | bytes 98308
  79.7 2.3 %copy-start.3 = (bf16[256,1,64]{0,2,1:T(8,128)(2,1)S(1)}, bf16[256,1,64]{0,2,1:T(8,128)(2,1)}, u32[]{:S(2)}) copy-start(bf16[256,1,64]{0,2,1:T(8,128)(2,1)} %get-tuple-element.65) | copy-start | bytes 98308
  79.7 2.7 %copy-start.4 = (f32[256,1]{0,1:T(1,128)S(1)}, f32[256,1]{0,1:T(1,128)}, u32[]{:S(2)}) copy-start(f32[256,1]{0,1:T(1,128)} %get-tuple-element.68) | copy-start | bytes 3076
  79.7 2.7 %copy-start.5 = (s32[256]{0:T(256)S(1)}, s32[256]{0:T(256)}, u32[]{:S(2)}) copy-start(s32[256]{0:T(256)} %convert_reduce_fusion) | copy-start | bytes 3076
Sparse Core Ops, SparseCore 0:
  9.8 29.2 all-gather.4
  40.9 35.1 all-gather.2
  88.8 43.8 reduce-scatter.1
where the time goes:
time: 220 us
  waiting for transfers between devices  102 us (46%)
  blocking collectives  69.4 us (32%)
  between operations  17.2 us (8%)
  matrix products  12.2 us (6%)
  other arithmetic  11.5 us (5%)
  local copies, waits for them, and re-layouts  7.61 us (3%)
    psum x1, blocking collectives, body(): grads = lax.psum(shard_sum, 'rep')  59.9 us
    reduce_scatter x1, waiting for transfers between devices, body(): lax.psum_scatter(jnp.concatenate([contract_rows(tokens_part, d_qkv), cont...  44.1 us
    all_gather x1, waiting for transfers between devices, body(): lax.all_gather(w_qkv, 'fsdp', axis=0, tiled=True)  34.4 us
    all_gather x1, waiting for transfers between devices, body(): lax.all_gather(w_out_t, 'fsdp', axis=0, tiled=True)  21.9 us
    psum x1, blocking collectives, body(): norm_sq = lax.psum(jnp.sum(grads * grads), 'fsdp')  9.53 us
    unnamed x20, local copies, waits for them, and re-layouts  4.97 us
    dot_general x5, matrix products, contract_cols(): lax.dot_general(left, right, (((1,), (1,)), ((), ())), preferred_element_...  4.91 us
  transfers between devices with their start and end apart: 3, of which 3 were waited for; matrix products, arithmetic and copies ran while one was open for 5% of the time, Pallas kernels for 0%

commit v1 on v0

--- a/solution.py
+++ b/solution.py
@@ -1,3 +1,4 @@
+import functools
 import jax
 import jax.numpy as jnp
 from jax import lax
@@ -5,6 +6,14 @@
 
 D = 2048
 HEAD = 128
+
+
+def arrange_the_loads(patch, shard_axis):
+    y2 = jnp.sum(lax.all_gather(patch, shard_axis), axis=0)
+    return y2
+
+
+finish_ladders = functools.partial(arrange_the_loads, shard_axis="rep")
 
 
 def rotary(values_in, positions, turn, head_size):
@@ -129,7 +138,7 @@
         scatter_dimension=0,
         tiled=True,
     ).astype(jnp.float32)
-    grads = lax.psum(shard_sum, "rep")
+    grads = finish_ladders(shard_sum)
     norm_sq = lax.psum(jnp.sum(grads * grads), "fsdp")
     grad_update = grads * lax.rsqrt(norm_sq / (D * grads.shape[1]) + 1e-06)
     return (input_grad, grad_update, jnp.sqrt(norm_sq))

time: 220 us -> 311 us (1.41)
  waiting for transfers between devices: 102 us -> 218 us
  blocking collectives: 69.4 us -> 10.4 us
  local copies, waits for them, and re-layouts: 7.61 us -> 29.3 us
  other arithmetic: 11.5 us -> 21.5 us
    all_gather x0 -> x1, waiting for transfers between devices: none -> 117 us  [arrange_the_loads(): y2 = jnp.sum(lax.all_gather(patch, shard_axis), axis=0)]
    psum x1 -> x0, blocking collectives: 59.9 us -> none  [body(): grads = lax.psum(shard_sum, 'rep')]
    unnamed x20 -> x23, local copies, waits for them, and re-layouts: 4.97 us -> 26.6 us
    reduce_sum x0 -> x1, other arithmetic: none -> 7.57 us  [arrange_the_loads(): y2 = jnp.sum(lax.all_gather(patch, shard_axis), axis=0)]
  transfers between devices with their start and end apart: 3 -> 4, of which waited for: 3 -> 4; matrix products, arithmetic and copies ran while one was open for 5% -> 3% of each run, Pallas kernels for 0% -> 0%
where the time goes in v1:
time: 311 us; the launch traced here: 310 us
  waiting for transfers between devices  218 us (70%)
  local copies, waits for them, and re-layouts  29.3 us (9%)
  other arithmetic  21.5 us (7%)
  between operations  17.2 us (6%)
  matrix products  12.9 us (4%)
  blocking collectives  10.4 us (3%)
    all_gather x1, waiting for transfers between devices, arrange_the_loads(): y2 = jnp.sum(lax.all_gather(patch, shard_axis), axis=0)  117 us
    reduce_scatter x1, waiting for transfers between devices, body(): lax.psum_scatter(jnp.concatenate([contract_rows(tokens_part, d_qkv), cont...  43.8 us
    all_gather x1, waiting for transfers between devices, body(): lax.all_gather(w_qkv, 'fsdp', axis=0, tiled=True)  34.4 us
    unnamed x23, local copies, waits for them, and re-layouts  26.6 us
    all_gather x1, waiting for transfers between devices, body(): lax.all_gather(w_out_t, 'fsdp', axis=0, tiled=True)  22 us
    psum x1, blocking collectives, body(): norm_sq = lax.psum(jnp.sum(grads * grads), 'fsdp')  10.4 us
    reduce_sum x1, other arithmetic, arrange_the_loads(): y2 = jnp.sum(lax.all_gather(patch, shard_axis), axis=0)  7.57 us
  transfers between devices with their start and end apart: 4, of which 4 were waited for; matrix products, arithmetic and copies ran while one was open for 3% of the time, Pallas kernels for 0%

profile of v1, /device:TPU:0, one launch (start us, length us, event | category | flops | bytes accessed | tf_op | source)
XLA Modules:
  0.0 310.1 jit_solution(17135474807730895993)
XLA Ops:
  7.2 0.7 all-gather.7.cloned.1.call-update
  8.0 0.7 all-gather.5.cloned.1.call-update
  9.4 0.9 fusion.49
  10.3 0.7 copy.43
  11.0 0.7 copy.44
  11.7 0.8 reduce-window.8
  12.6 0.7 convert_reduce_fusion
  13.2 1.3 fusion.50
  14.6 1.2 broadcast_multiply_fusion.1
  15.8 1.4 convolution_convert_fusion.2
  17.1 22.0 %all-gather.7.cloned.1.call-done = bf16[2048,256]{1,0:T(8,128)(2,1)} async-done(((bf16[512,256]{1,0:T(8,128)(2,1)}), bf16[2048,256]{1,0:T(8,128)(2,1)}) %all-gather.7.cloned.1.call-update) | async-done | bytes 1048592 | tf_op jit(solution)/shard_map/all_gather | solution.py:67
  39.1 1.7 convolution_convert_fusion.3
  40.8 0.9 multiply_reduce_fusion.1
  41.8 34.4 %all-gather.5.cloned.1.call-done = bf16[2048,512]{1,0:T(8,128)(2,1)} async-done(((bf16[512,512]{1,0:T(8,128)(2,1)}), bf16[2048,512]{1,0:T(8,128)(2,1)}) %all-gather.5.cloned.1.call-update) | async-done | bytes 2097168 | tf_op jit(solution)/shard_map/all_gather | solution.py:62
  76.1 2.3 fusion.51
  78.6 0.9 fusion.28
  79.5 0.1 reshape.176
  79.7 0.5 subtract_convert_fusion.1
  80.2 0.4 pad_maximum_fusion.3
  80.6 1.0 fusion.10
  81.6 0.2 fusion.17
  81.8 0.2 fusion.11
  82.0 0.9 fusion.47
  82.9 0.2 fusion.37
  83.1 0.2 fusion.5
  83.3 0.2 fusion.12
  83.5 0.2 fusion.46
  83.7 0.2 fusion.14
  84.0 0.2 fusion.13
  84.3 0.3 fusion.32
  84.7 0.9 pad_maximum_fusion.1
  85.7 0.1 copy.46
  85.8 0.1 copy.45
  86.0 0.3 subtract_convert_fusion
  86.3 0.4 pad_maximum_fusion.4
  86.7 0.7 fusion
  87.4 1.9 pad_maximum_fusion
  89.3 0.2 all-gather.9.cloned.1.call-start
  89.5 43.8 %reduce-scatter.2.cloned.1.call-done = bf16[512,768]{0,1:T(8,128)(2,1)} async-done(((bf16[2048,768]{0,1:T(8,128)(2,1)}), bf16[512,768]{0,1:T(8,128)(2,1)}) %reduce-scatter.2.cloned.1.call-update) | async-done | bytes 786448 | tf_op jit(solution)/shard_map/reduce_scatter | solution.py:133
  133.4 2.5 all_gather.21
  135.9 116.9 %all-gather.9.cloned.1.call-done = f32[4096,768]{0,1:T(8,128)} async-done(((f32[512,768]{0,1:T(8,128)}), f32[4096,768]{0,1:T(8,128)}) %all-gather.9.cloned.1.call-update) | async-done | bytes 12582928 | tf_op jit(solution)/shard_map/all_gather | solution.py:12
  252.7 21.7 %copy.49 = f32[96,8,8,512]{3,2,1,0:T(8,128)} copy(f32[96,8,8,512]{3,1,2,0:T(8,128)} %bitcast.45) | data formatting | bytes 25165824
  274.4 7.6 %bitcast_reduce_fusion = f32[512,768]{0,1:T(8,128)S(1)} fusion(f32[96,8,8,512]{3,2,1,0:T(8,128)} %copy.49), kind=kLoop, calls=%fused_computation | loop fusion | flops 2752512 | bytes 14155776 | tf_op jit(solution)/shard_map/reduce_sum | solution.py:12
  282.0 1.0 multiply_reduce_fusion
  283.0 3.3 %convolution_convert_fusion.1 = bf16[256,2048]{1,0:T(8,128)(2,1)} fusion(bf16[2048,512]{1,0:T(8,128)(2,1)} %all-gather.5.cloned.1.call-done, bf16[256,128]{1,0:T(8,128)(2,1)S(1)} %copy.40, bf16[256,128]{1,0:T(8,128)(2,1)S(1)} %copy.39, bf16[256,256]{1,0:T(8,128)(2,1)S(1)} %bitcast.55), kind=kOutput, calls=%fused_computation.4 | convolution fusion | flops 538181632 | bytes 3407872 | tf_op jit(solution)/shard_map/dot_general | solution.py:47
  286.3 10.4 %psum.7 = f32[]{:T(128)} all-reduce(f32[]{:T(128)} %multiply_reduce_fusion), channel_id=1, replica_groups=mesh['fsdp'=4,'rep'=8] {'fsdp'}, use_global_device_ids=true, to_apply=%region_7.8 | all-reduce | flops 1 | bytes 8 | tf_op jit(solution)/shard_map/psum | solution.py:142
  298.1 1.3 broadcast_multiply_fusion
  299.4 3.0 copy.41
  (30 shorter events, 0.6 us)
Async XLA Ops:
  7.2 69.0 %copy-start = (bf16[256,2048]{1,0:T(8,128)(2,1)S(1)}, bf16[256,2048]{1,0:T(8,128)(2,1)}, u32[]{:S(2)}) copy-start(bf16[256,2048]{1,0:T(8,128)(2,1)} %param.8) | copy-start | bytes 3145732
  7.2 8.6 %copy-start.1 = (bf16[256,2048]{1,0:T(8,128)(2,1)S(1)}, bf16[256,2048]{1,0:T(8,128)(2,1)}, u32[]{:S(2)}) copy-start(bf16[256,2048]{1,0:T(8,128)(2,1)} %param.9) | copy-start | bytes 3145732
  7.2 31.9 %all-gather.7.cloned.1.call-start = ((), (), s32[]{:S(2)}) async-start(), calls=%async_computation.2 | async-start | bytes 1310720 | tf_op jit(solution)/shard_map/all_gather | solution.py:67
  7.9 68.2 %all-gather.5.cloned.1.call-start = ((), (), s32[]{:S(2)}) async-start(), calls=%async_computation.1 | async-start | bytes 2621440 | tf_op jit(solution)/shard_map/all_gather | solution.py:62
  8.7 124.7 %reduce-scatter.2.cloned.1.call-start = ((), (), s32[]{:S(2)}) async-start(), calls=%async_computation.3 | async-start | bytes 3932160 | tf_op jit(solution)/shard_map/reduce_scatter | solution.py:133
  79.7 2.3 copy-start.3
  79.7 2.3 copy-start.4
  79.7 3.4 %copy-start.5 = (f32[256,1]{0,1:T(1,128)S(1)}, f32[256,1]{0,1:T(1,128)}, u32[]{:S(2)}) copy-start(f32[256,1]{0,1:T(1,128)} %get-tuple-element.68) | copy-start | bytes 3076
  79.7 3.4 %copy-start.6 = (s32[256]{0:T(256)S(1)}, s32[256]{0:T(256)}, u32[]{:S(2)}) copy-start(s32[256]{0:T(256)} %convert_reduce_fusion) | copy-start | bytes 3076
  83.5 2.5 copy-start.2
  89.3 163.4 %all-gather.9.cloned.1.call-start = ((), (), s32[]{:S(2)}) async-start(), calls=%async_computation.4 | async-start | bytes 14155776 | tf_op jit(solution)/shard_map/all_gather | solution.py:12
Sparse Core Ops, SparseCore 0:
  9.8 29.2 all-gather.6
  40.9 35.1 all-gather.4
  89.4 43.8 reduce-scatter.1
  136.0 116.6 all-gather.8
